TPU v7x, 32 devices: a 4x2x2 block of a 4x4x8 slice. The times are simulated.
32 devices in a mesh: dp: 4 (over y, z), tp: 8 (over x, core).
Axes of the slice: x: 4, y: 2, z: 2, core: 2. Of those that a mesh axis runs over, the one named last changes fastest.
The devices are a block of a 4x4x8 slice.
Arguments:
- token_ids: int32 [32768], P('dp'), parts along dimension 0
- positions: int32 [32768], P('dp'), parts along dimension 0
- embed_table: bfloat16 [257216, 2048], P('tp')
- norm_scale: float32 [2048], replicated
- w_query: bfloat16 [2048, 2048], P(None, 'tp')
- w_key: bfloat16 [2048, 256], replicated
- w_value: bfloat16 [2048, 256], replicated
Outputs:
- output 1: bfloat16 [32768, 2048], P(('dp', 'tp')), parts along dimension 0
- output 2: bfloat16 [32768, 8, 256], P('dp', 'tp'), parts along dimension 0
- output 3: bfloat16 [32768, 8, 256], P('dp', 'tp'), parts along dimension 0
- output 4: bfloat16 [32768, 8, 256], P('dp', 'tp'), parts along dimension 0
There are 4 independent parts. A program takes and returns all parts, laid end to end along the dimension named above; an argument that names none is the same for every part.
All inputs are finite; a program needn't handle non-finite values.
Results may differ from a plain program's by a relative error of at most 0.0120276.
Values are sent between devices in bfloat16 or wider.
A program may use at most 768 MiB of HBM per device.

v0:
```python
import functools
import math
import jax
import jax.numpy as jnp
import numpy as np
from jax import lax
from jax.experimental import pallas as pl
from jax.experimental.pallas import tpu as pltpu
from jax.sharding import PartitionSpec as P

HEAD_DIM = 256
EPSILON = 1e-6
ROPE_BASE = 10000.0
CHUNK = 64
PICK = 64
SLAB = 8
DEPTH = 4
CORES = 2
VMEM_LIMIT = 60 * 1024 * 1024


def inverse_freq():
    return ROPE_BASE ** (-jnp.arange(0, HEAD_DIM, 2, dtype=jnp.float32) / HEAD_DIM)


def rope_tables(positions):
    angles = positions.astype(jnp.float32)[:, None] * inverse_freq()[None, :]
    return jnp.cos(angles), jnp.sin(angles)


def rms_norm(resid_rows, norm_scale):
    widened = resid_rows.astype(jnp.float32)
    inv_rms = lax.rsqrt(jnp.mean(widened * widened, axis=-1, keepdims=True) + EPSILON)
    return (widened * inv_rms * (1.0 + norm_scale)).astype(jnp.bfloat16)


def rotate(head_vals, cosines, sines):
    half_dim = head_vals.shape[-1] // 2
    front_half = head_vals[..., :half_dim]
    back_half = head_vals[..., half_dim:]
    return jnp.concatenate([front_half * cosines - back_half * sines, back_half * cosines + front_half * sines], axis=-1)


def project(normed, weight, cosines, sines, factor):
    linear = jnp.dot(normed, weight, preferred_element_type=jnp.float32).astype(jnp.bfloat16)
    head_view = linear.reshape(linear.shape[0], -1, HEAD_DIM).astype(jnp.float32)
    return (rotate(head_view, cosines, sines) * factor).astype(jnp.bfloat16)


def dense_path(group_size, token_ids, positions, table_rows, norm_scale, w_query, key_cols, value_cols):
    dev_index = lax.axis_index("tp")
    vocab_rows, model_width = table_rows.shape
    normalizer = jnp.asarray(math.sqrt(model_width), dtype=jnp.bfloat16)
    local_ids = token_ids - dev_index * vocab_rows
    inside = (local_ids >= 0) & (local_ids < vocab_rows)
    picked = jnp.take(table_rows, local_ids, axis=0, mode="clip") * normalizer
    partial = jnp.where(inside[:, None], picked, jnp.zeros((), jnp.bfloat16))
    by_owner = partial.reshape(group_size, -1, model_width)
    residual = jnp.sum(lax.all_to_all(by_owner, "tp", 0, 0), axis=0)
    normed = rms_norm(residual, norm_scale)
    copies = jnp.broadcast_to(normed[None], (group_size, *normed.shape))
    normed = lax.all_to_all(copies, "tp", 0, 0).reshape(-1, model_width)
    cosines, sines = rope_tables(positions)
    cosines, sines = cosines[:, None, :], sines[:, None, :]
    queries = project(normed, w_query, cosines, sines, HEAD_DIM ** -0.5)
    key_heads = project(normed, key_cols, cosines, sines, 1.0)
    value_lin = jnp.dot(normed, value_cols, preferred_element_type=jnp.float32).astype(jnp.bfloat16)
    return residual, queries[:, 0, :], key_heads[:, 0, :], value_lin


class Plan:
    def __init__(self, group_size, tokens, vocab_rows):
        unit = CHUNK * 2
        self.hot = min(tokens // 8, vocab_rows // unit * unit)
        share = [11 / 32, 5 / 64] + [3 / 64] * 2
        room = [share[o] if o < 4 else 3 / 128 for o in range(group_size)]
        self.caps = [max(CHUNK, -(-int(tokens * r) // CHUNK) * CHUNK) for r in room]
        self.bases, at = [], self.hot
        for cap in self.caps:
            self.bases.append(at)
            at += cap
        self.rows = at
        self.list_rows = -(-(-(-max(self.caps) // 128)) // 8) * 8


def choose(values, index):
    out = jnp.int32(values[0])
    for j in range(1, len(values)):
        out = jnp.where(index == j, jnp.int32(values[j]), out)
    return out


def offsets_by_column(rows):
    offsets = (rows & (SLAB - 1)).astype(jnp.float32)
    fill = jnp.zeros((128 - rows.shape[0], 128), jnp.float32)
    return jnp.concatenate([offsets, fill], axis=0).T


def prep_kernel(plan, group_size, vocab_rows, ids_ref, slot_ref, list_ref, count_ref, offset_ref, over_ref):
    me = lax.axis_index("tp")
    ids = ids_ref[...]
    blocks, lanes = ids.shape
    cold = ids >= plan.hot
    masks = [cold & (ids >= o * vocab_rows) & (ids < (o + 1) * vocab_rows) for o in range(group_size)]
    stack = jnp.concatenate([m.astype(jnp.float32) for m in masks], axis=0)
    stack = stack.astype(jnp.bfloat16)
    tri_r = lax.broadcasted_iota(jnp.int32, (lanes, lanes), 0)
    tri_c = lax.broadcasted_iota(jnp.int32, (lanes, lanes), 1)
    upper = (tri_r <= tri_c).astype(jnp.float32).astype(jnp.bfloat16)
    within = jnp.dot(stack, upper, preferred_element_type=jnp.float32)
    totals = jnp.dot(stack, jnp.ones((lanes, lanes), jnp.bfloat16), preferred_element_type=jnp.float32)
    low_r = lax.broadcasted_iota(jnp.int32, (blocks, blocks), 0)
    low_c = lax.broadcasted_iota(jnp.int32, (blocks, blocks), 1)
    lower = (low_c < low_r).astype(jnp.float32).astype(jnp.bfloat16)
    slot = jnp.where(cold, 0, ids)
    own_rank = jnp.full((blocks, lanes), -1, jnp.int32)
    over = jnp.zeros((1, lanes), jnp.int32)
    for o in range(group_size):
        tot = totals[o * blocks:(o + 1) * blocks]
        before = jnp.dot(lower, tot.astype(jnp.bfloat16), preferred_element_type=jnp.float32)
        rank = (before + within[o * blocks:(o + 1) * blocks]).astype(jnp.int32) - 1
        slot = slot + jnp.where(masks[o], jnp.minimum(rank, plan.caps[o] - 1) + plan.bases[o], 0)
        own_rank = jnp.where(masks[o] & (me == o), rank, own_rank)
        count = (before[blocks - 1:] + tot[blocks - 1:]).astype(jnp.int32)
        count_ref[o:o + 1, :] = count
        over = jnp.maximum(over, count - plan.caps[o])
    slot_ref[...] = slot
    over_ref[0] = jnp.max(over)
    local = jnp.where(own_rank >= 0, ids - me * vocab_rows, 0)
    major, minor = own_rank >> 7, own_rank & 127
    high, low = local >> 8, local & 255
    iota_major = lax.broadcasted_iota(jnp.int32, (plan.list_rows, lanes), 0)
    iota_minor = lax.broadcasted_iota(jnp.int32, (lanes, lanes), 0)
    acc = jnp.zeros((2 * plan.list_rows, lanes), jnp.float32)
    per = 8
    for g in range(blocks // per):
        lhs, rhs = [], []
        for r in range(g * per, (g + 1) * per):
            hit = iota_major == major[r:r + 1, :]
            lhs.append(jnp.concatenate([jnp.where(hit, high[r:r + 1, :], 0), jnp.where(hit, low[r:r + 1, :], 0)], axis=0).astype(jnp.float32))
            rhs.append((iota_minor == minor[r:r + 1, :]).astype(jnp.float32))
        left = jnp.concatenate(lhs, axis=1).astype(jnp.bfloat16)
        right = jnp.concatenate(rhs, axis=1).astype(jnp.bfloat16)
        acc = acc + lax.dot_general(left, right, (((1,), (1,)), ((), ())), preferred_element_type=jnp.float32)
    whole = acc.astype(jnp.int32)
    wanted = whole[:plan.list_rows] * 256 + whole[plan.list_rows:]
    list_ref[...] = wanted
    offset_ref[...] = offsets_by_column(wanted)


def prepare(plan, group_size, vocab_rows, token_ids):
    blocks = token_ids.shape[0] // 128
    return pl.pallas_call(
        functools.partial(prep_kernel, plan, group_size, vocab_rows),
        out_shape=(
            jax.ShapeDtypeStruct((blocks, 128), jnp.int32),
            jax.ShapeDtypeStruct((plan.list_rows, 128), jnp.int32),
            jax.ShapeDtypeStruct((group_size, 128), jnp.int32),
            jax.ShapeDtypeStruct((128, 128), jnp.float32),
            jax.ShapeDtypeStruct((1,), jnp.int32),
        ),
        out_specs=[pl.BlockSpec(memory_space=pltpu.VMEM)] * 4 + [pl.BlockSpec(memory_space=pltpu.SMEM)],
        compiler_params=pltpu.CompilerParams(vmem_limit_bytes=VMEM_LIMIT),
        name="slots",
    )(token_ids.reshape(blocks, 128))


class Picker:
    def __init__(self, rows_smem, begin, groups, offsets, source, slabs, sem):
        self.rows_smem, self.begin, self.groups = rows_smem, begin, groups
        self.offsets, self.source, self.slabs, self.sem = offsets, source, slabs, sem

    def fetch(self, g):
        place = lax.rem(jnp.int32(g), DEPTH)
        first = self.begin + jnp.minimum(g, jnp.maximum(self.groups - 1, 0)) * PICK
        for i in range(PICK):
            row = self.rows_smem[first + i]
            start = pl.multiple_of((row >> 3) << 3, SLAB)
            pltpu.make_async_copy(self.source.at[pl.ds(start, SLAB)], self.slabs.at[place, pl.ds(i * SLAB, SLAB)], self.sem.at[place]).start()

    def wait(self, g):
        place = lax.rem(jnp.int32(g), DEPTH)
        pltpu.make_async_copy(self.source.at[pl.ds(0, PICK * SLAB)], self.slabs.at[place], self.sem.at[place]).wait()

    def pick(self, g):
        place = lax.rem(jnp.int32(g), DEPTH)
        per = 128 // PICK
        block = self.offsets[pl.ds(pl.multiple_of(lax.rem(g, per) * PICK, PICK), PICK), :]
        lane = lax.broadcasted_iota(jnp.int32, (PICK, 128), 1)
        column = jnp.sum(jnp.where(lane == lax.div(g, per), block, 0.0), axis=1, keepdims=True).astype(jnp.int32)
        shape = (PICK, PICK * SLAB)
        hit = lax.broadcasted_iota(jnp.int32, shape, 1) == lax.broadcasted_iota(jnp.int32, shape, 0) * SLAB + column
        onehot = jnp.where(hit, 1.0, 0.0).astype(jnp.bfloat16)
        return jnp.dot(onehot, self.slabs[place], preferred_element_type=jnp.float32)

    def lead(self):
        for g in range(DEPTH - 1):
            self.fetch(g)

    def turn(self, g):
        self.wait(g)
        self.fetch(g + DEPTH - 1)
        return self.pick(g)

    def drain(self, groups):
        for g in range(DEPTH - 1):
            self.wait(groups + g)


def gather_kernel(plan, normalizer, counts, rows_smem, offsets, table, out, slabs, stage, hot_in, hot_out, sem, out_sem, hot_sem):
    me = lax.axis_index("tp")
    total = jnp.minimum(counts[me, 0], choose(plan.caps, me))
    base = choose(plan.bases, me)
    scale = jnp.float32(normalizer)
    groups = (total + PICK - 1) // PICK
    picker = Picker(rows_smem, 0, groups, offsets, table, slabs, sem)
    picker.lead()

    def emit(g, picked):
        side = lax.rem(g, 2)

        @pl.when(g >= 2)
        def _():
            pltpu.make_async_copy(stage.at[side], out.at[pl.ds(0, PICK)], out_sem.at[side]).wait()

        stage[side] = (picked * scale).astype(jnp.bfloat16)
        at = pl.multiple_of(base + g * PICK, PICK)
        pltpu.make_async_copy(stage.at[side], out.at[pl.ds(at, PICK)], out_sem.at[side]).start()

    step = hot_in.shape[1]
    hot_steps = jnp.where(me == 0, plan.hot // step, 0)

    def load(i):
        return pltpu.make_async_copy(table.at[pl.ds(pl.multiple_of(i * step, step), step)], hot_in.at[lax.rem(i, 2)], hot_sem.at[lax.rem(i, 2)])

    def save(i):
        return pltpu.make_async_copy(hot_out.at[lax.rem(i, 2)], out.at[pl.ds(pl.multiple_of(i * step, step), step)], hot_sem.at[2 + lax.rem(i, 2)])

    def hot_turn(i):
        @pl.when(i < hot_steps)
        def _():
            load(i).wait()

            @pl.when(i >= 2)
            def _():
                save(i - 2).wait()
            hot_out[lax.rem(i, 2)] = (hot_in[lax.rem(i, 2)].astype(jnp.float32) * scale).astype(jnp.bfloat16)
            save(i).start()

            @pl.when(i + 2 < hot_steps)
            def _():
                load(i + 2).start()

    for i in range(2):
        @pl.when(i < hot_steps)
        def _():
            load(jnp.int32(i)).start()

    def rest(i, carry):
        hot_turn(i)
        return carry

    def body(g, carry):
        emit(g, picker.turn(g))
        hot_turn(g)
        return carry

    lax.fori_loop(0, groups, body, 0)
    lax.fori_loop(groups, jnp.maximum(hot_steps, groups), rest, 0)
    picker.drain(groups)
    for back in (2, 1):
        @pl.when(hot_steps >= back)
        def _():
            save(hot_steps - back).wait()
    for last in (2, 1):
        @pl.when(groups >= last)
        def _():
            side = lax.rem(groups - last, 2)
            pltpu.make_async_copy(stage.at[side], out.at[pl.ds(0, PICK)], out_sem.at[side]).wait()


def gather_rows(plan, normalizer, counts, rows, offsets, table):
    width = table.shape[1]
    hot_step = CHUNK
    return pl.pallas_call(
        functools.partial(gather_kernel, plan, normalizer),
        out_shape=jax.ShapeDtypeStruct((plan.rows, width), table.dtype),
        in_specs=[pl.BlockSpec(memory_space=pltpu.SMEM), pl.BlockSpec(memory_space=pltpu.SMEM), pl.BlockSpec(memory_space=pltpu.VMEM), pl.BlockSpec(memory_space=pl.ANY)],
        out_specs=pl.BlockSpec(memory_space=pl.ANY),
        scratch_shapes=[
            pltpu.VMEM((DEPTH, PICK * SLAB, width), table.dtype),
            pltpu.VMEM((2, PICK, width), table.dtype),
            pltpu.VMEM((2, hot_step, width), table.dtype),
            pltpu.VMEM((2, hot_step, width), table.dtype),
            pltpu.SemaphoreType.DMA((DEPTH,)),
            pltpu.SemaphoreType.DMA((2,)),
            pltpu.SemaphoreType.DMA((4,)),
        ],
        compiler_params=pltpu.CompilerParams(vmem_limit_bytes=VMEM_LIMIT),
        cost_estimate=pl.CostEstimate(flops=2 * 2048 * 256 * 2816, bytes_accessed=100_000_000, transcendentals=0),
        name="owner_rows",
    )(counts, rows, offsets, table)


TOK = 512
SUB = 32
UNROLL = 4
TURN = 256
LAG = 2
HALF_PI = (1.5703125, 4.837512969970703e-4, 7.549789948768648e-8)
SIN_POLY = (-1.6666654611e-1, 8.3321608736e-3, -1.9515295891e-4)
COS_POLY = (4.166664568298827e-2, -1.388731625493765e-3, 2.443315711809948e-5)


def cos_sin(angles):
    turns = jnp.floor(angles * (2 / math.pi) + 0.5)
    x = angles - turns * HALF_PI[0]
    x = x - turns * HALF_PI[1]
    x = x - turns * HALF_PI[2]
    x2 = x * x
    sine = x + x * x2 * (SIN_POLY[0] + x2 * (SIN_POLY[1] + x2 * SIN_POLY[2]))
    cosine = 1.0 - 0.5 * x2 + x2 * x2 * (COS_POLY[0] + x2 * (COS_POLY[1] + x2 * COS_POLY[2]))
    quarter = turns.astype(jnp.int32)
    swap = (quarter & 1) == 1
    first, second = jnp.where(swap, sine, cosine), jnp.where(swap, cosine, sine)
    return jnp.where(((quarter + 1) & 2) == 2, -first, first), jnp.where((quarter & 2) == 2, -second, second)


def multicast_kernel(plan, group_size, buf_in, scale_ref, wq_ref, wk_ref, wv_ref, pos_ref, freq_ref, buf, lin, tiles, cos_out, sin_out, got, ring_sem, pair_sem, fresh, made, wide, tiled, turned, in_sem, out_sem, tile_sem, turn_sem):
    del buf_in
    chips = group_size // CORES
    me = lax.axis_index("tp")
    chip, core = lax.div(me, CORES), lax.rem(me, CORES)
    mate = chip * CORES + (1 - core)
    step = 1 - 2 * core

    def chip_at(delta):
        return lax.rem(chip + delta * step + 2 * chips, chips)

    ahead, behind = chip_at(1) * CORES + core, chip_at(-1) * CORES + core

    barrier = pltpu.get_barrier_semaphore()
    for other in (mate, ahead, behind):
        pl.semaphore_signal(barrier, inc=1, device_id={"tp": other}, device_id_type=pl.DeviceIdType.MESH)
    pl.semaphore_wait(barrier, 3)

    own_n = [c // CHUNK for c in plan.caps]
    own_n[0] += plan.hot // CHUNK
    own_at, at = [], 0
    for c in own_n:
        own_at.append(at)
        at += c
    first = [own_at[2 * c] for c in range(chips)]
    half = [(own_n[2 * c] + own_n[2 * c + 1]) // 2 for c in range(chips)]
    turn = [own_n[2 * c] - half[c] for c in range(chips)]

    def rows(j):
        return pl.ds(pl.multiple_of(j * CHUNK, CHUNK), CHUNK)

    def ring(j):
        return pltpu.make_async_remote_copy(src_ref=buf.at[rows(j)], dst_ref=buf.at[rows(j)], send_sem=ring_sem.at[j], recv_sem=got.at[j], device_id={"tp": ahead}, device_id_type=pl.DeviceIdType.MESH)

    def pair(j):
        return pltpu.make_async_remote_copy(src_ref=buf.at[rows(j)], dst_ref=buf.at[rows(j)], send_sem=pair_sem.at[j], recv_sem=got.at[j], device_id={"tp": mate}, device_id_type=pl.DeviceIdType.MESH)

    def loop(count, fn):
        def body(t, c):
            fn(t)
            return c
        lax.fori_loop(0, count, body, 0)

    my_first, my_half, my_turn = choose(first, chip), choose(half, chip), choose(turn, chip)
    mine = jnp.where(core == 0, my_half, my_half - my_turn)
    mine_at = jnp.where(core == 0, my_first, my_first + my_half + my_turn)
    cross_at = my_first + my_half

    @pl.when(core == 0)
    def _():
        loop(my_turn, lambda t: pair(cross_at + t).start())

    loop(mine, lambda t: ring(mine_at + t).start())
    loop(mine, lambda t: pair(mine_at + t).start())

    @pl.when(core == 1)
    def _():
        def relay(t):
            pair(cross_at + t).wait_recv()
            ring(cross_at + t).start()
        loop(my_turn, relay)

    def arrival(t, way, ring_core):
        chunk, hops, at = jnp.int32(0), jnp.int32(1), jnp.int32(0)
        for hop in range(1, chips):
            origin = lax.rem(chip - hop * way + 2 * chips, chips)
            count = choose(half, origin)
            here = choose(first, origin) + ring_core * count + lax.rem(jnp.maximum(t - at, 0) + ring_core * choose(turn, origin), count)
            chunk = jnp.where(t >= at, here, chunk)
            hops = jnp.where(t >= at, hop, hops)
            at = at + count
        return chunk, hops

    both = my_half * 2
    rot = core * (my_half + my_turn)
    width = 2 * CHUNK

    def home(s, side):
        return my_first + lax.rem(2 * s + side + rot, both)

    def chunks_of(s):
        t = jnp.maximum(s - my_half, 0)
        local = s < my_half
        come, _ = arrival(t, step, core)
        cross, _ = arrival(t, -step, 1 - core)
        return jnp.where(local, home(s, 0), come), jnp.where(local, home(s, 1), cross)

    def load(s, side, j):
        place = lax.rem(s, 2)
        return pltpu.make_async_copy(buf.at[rows(j)], fresh.at[place, pl.ds(side * CHUNK, CHUNK)], in_sem.at[place, side])

    def save(s, side, j):
        place = lax.rem(s, 2)
        at = pl.multiple_of(j * (CHUNK * 8), CHUNK * 8)
        return pltpu.make_async_copy(made.at[place, pl.ds(side * CHUNK * 8, CHUNK * 8)], lin.at[pl.ds(at, CHUNK * 8)], out_sem.at[place, side])

    per_row = tiles.shape[0] // plan.rows

    def lay(s, side, j):
        place = lax.rem(s, 2)
        at = pl.multiple_of(j * (CHUNK * per_row), CHUNK * per_row)
        return pltpu.make_async_copy(tiled.at[place, pl.ds(side * CHUNK * per_row, CHUNK * per_row)], tiles.at[pl.ds(at, CHUNK * per_row)], tile_sem.at[place, side])

    def compute(s):
        place = lax.rem(s, 2)
        one, two = chunks_of(s)
        load(s, 0, one).wait()
        load(s, 1, two).wait()

        @pl.when(s >= 2)
        def _():
            save(s, 0, 0).wait()
            save(s, 1, 0).wait()
            lay(s, 0, 0).wait()
            lay(s, 1, 0).wait()
        came = fresh[place]
        for j in range(per_row):
            wide[pl.ds(j, width, stride=per_row), :] = came[:, j * 128:(j + 1) * 128].astype(jnp.float32)
        tiled[place] = wide[...].astype(tiled.dtype)
        lay(s, 0, one).start()
        lay(s, 1, two).start()
        normed = rms_norm(came, scale_ref[...])
        at = 0
        for w in (wq_ref, wk_ref, wv_ref):
            y = jnp.dot(normed, w[...], preferred_element_type=jnp.float32).astype(jnp.bfloat16).astype(jnp.float32)
            for j in range(y.shape[1] // 128):
                made[place, pl.ds(at, width, stride=8), :] = y[:, j * 128:(j + 1) * 128]
                at += 1
        save(s, 0, one).start()
        save(s, 1, two).start()

    lines, span = TURN // 128, TURN
    blocks = pos_ref.shape[0] // lines

    def keep(s, which):
        place = lax.rem(s, 2)
        at = pl.multiple_of(s * span, span)
        return pltpu.make_async_copy(turned.at[place, which], (cos_out, sin_out)[which].at[pl.ds(at, span)], turn_sem.at[place, which])

    def tables(s):
        place = lax.rem(s, 2)

        @pl.when(s >= 2)
        def _():
            for which in range(2):
                keep(s - 2, which).wait()
        pos = jnp.concatenate([pos_ref[pl.ds(s * lines + i, 1), :] for i in range(lines)], axis=1)
        sub = lax.broadcasted_iota(jnp.int32, (16, span), 0)
        digits = jnp.where(sub == 0, (pos >> 7) << 7, jnp.where(sub == 1, pos & 127, 0))
        digits = digits.astype(jnp.float32).astype(jnp.bfloat16)
        ones = jnp.ones((16, freq_ref.shape[1]), jnp.bfloat16)
        spread = lax.dot_general(digits, ones, (((0,), (0,)), ((), ())), preferred_element_type=jnp.float32)
        cosines, sines = cos_sin(spread * freq_ref[...])
        turned[place, 0] = cosines
        turned[place, 1] = sines
        for which in range(2):
            keep(s, which).start()

    def turn_of(s, carry):
        one, two = chunks_of(s)
        for side, j in ((0, one), (1, two)):
            place = j - my_first
            unseen = jnp.where(core == 0, place >= my_half + my_turn, place < my_half)

            @pl.when((s < my_half) & unseen)
            def _():
                pair(j).wait_recv()

        @pl.when(s >= my_half)
        def _():
            _, hops = arrival(s - my_half, step, core)
            ring(one).wait_recv()

            @pl.when(hops < chips - 1)
            def _():
                ring(one).start()
            pair(one).start()
            pair(two).wait_recv()
        load(s, 0, one).start()
        load(s, 1, two).start()

        @pl.when(s >= 1)
        def _():
            compute(s - 1)

        @pl.when(s < blocks)
        def _():
            tables(s)
        return carry

    rounds = plan.rows // CHUNK // 2
    assert 2 <= blocks <= rounds
    lax.fori_loop(0, rounds, turn_of, 0)
    compute(jnp.int32(rounds - 1))
    for s in (rounds - 2, rounds - 1):
        for side in range(2):
            save(jnp.int32(s), side, 0).wait()
            lay(jnp.int32(s), side, 0).wait()
    for s in (blocks - 2, blocks - 1):
        for which in range(2):
            keep(jnp.int32(s), which).wait()

    @pl.when(core == 0)
    def _():
        loop(my_turn, lambda t: pair(cross_at + t).wait_send())

    @pl.when(core == 1)
    def _():
        loop(my_turn, lambda t: ring(cross_at + t).wait_send())

    def sent(t):
        ring(mine_at + t).wait_send()
        pair(mine_at + t).wait_send()
    loop(mine, sent)
    for hop in range(1, chips):
        origin = chip_at(-hop)
        count = choose(half, origin)
        base = choose(first, origin) + core * count

        def left(t):
            if hop < chips - 1:
                ring(base + t).wait_send()
            pair(base + t).wait_send()
        loop(count, left)


def multicast(plan, group_size, buf, norm_scale, w_query, key_cols, value_cols, positions):
    chunks, width = plan.rows // CHUNK, buf.shape[1]
    per_row = width // 128
    tokens, half = positions.shape[0], HEAD_DIM // 2
    table = jax.ShapeDtypeStruct((tokens, half), jnp.float32)
    vmem = pl.BlockSpec(memory_space=pltpu.VMEM)
    return pl.pallas_call(
        functools.partial(multicast_kernel, plan, group_size),
        out_shape=(jax.ShapeDtypeStruct(buf.shape, buf.dtype), jax.ShapeDtypeStruct((plan.rows * 8, 128), jnp.float32), jax.ShapeDtypeStruct((plan.rows * per_row, 128), buf.dtype), table, table),
        in_specs=[pl.BlockSpec(memory_space=pl.ANY)] + [vmem] * 6,
        out_specs=(pl.BlockSpec(memory_space=pl.ANY),) * 5,
        scratch_shapes=[
            pltpu.SemaphoreType.DMA((chunks,)),
            pltpu.SemaphoreType.DMA((chunks,)),
            pltpu.SemaphoreType.DMA((chunks,)),
            pltpu.VMEM((2, 2 * CHUNK, width), buf.dtype),
            pltpu.VMEM((2, 2 * CHUNK * 8, 128), jnp.float32),
            pltpu.VMEM((2 * CHUNK * per_row, 128), jnp.float32),
            pltpu.VMEM((2, 2 * CHUNK * per_row, 128), buf.dtype),
            pltpu.VMEM((2, 2, TURN, half), jnp.float32),
            pltpu.SemaphoreType.DMA((2, 2)),
            pltpu.SemaphoreType.DMA((2, 2)),
            pltpu.SemaphoreType.DMA((2, 2)),
            pltpu.SemaphoreType.DMA((2, 2)),
        ],
        input_output_aliases={0: 0},
        compiler_params=pltpu.CompilerParams(collective_id=0, has_side_effects=True, vmem_limit_bytes=VMEM_LIMIT),
        cost_estimate=pl.CostEstimate(flops=100_000_000_000, bytes_accessed=100_000_000, transcendentals=0),
        name="multicast",
    )(buf, norm_scale.reshape(1, width), w_query, key_cols, value_cols, positions.reshape(-1, 128), inverse_freq().reshape(1, half))


def expand_kernel(lag, slots, lin, tiles, cos_ref, sin_ref, r_ref, q_ref, k_ref, v_ref, store, spread, raw, wide, sem, fetch_sem):
    step, steps = pl.program_id(0), pl.num_programs(0) - lag
    me = lax.axis_index("tp")
    whole = pltpu.make_async_copy(lin, store, sem)
    count, width = r_ref.shape
    per_row = width // 128

    def fetch(g):
        place = lax.rem(jnp.int32(g), DEPTH)
        first = (me * steps + jnp.minimum(g, steps - 1)) * count
        for i in range(count):
            at = pl.multiple_of(slots[first + i] * per_row, per_row)
            pltpu.make_async_copy(tiles.at[pl.ds(at, per_row)], raw.at[place, pl.ds(i * per_row, per_row)], fetch_sem.at[place]).start()

    def arrived(g):
        place = lax.rem(jnp.int32(g), DEPTH)
        pltpu.make_async_copy(tiles.at[pl.ds(0, count * per_row)], raw.at[place], fetch_sem.at[place]).wait()

    @pl.when(step == 0)
    def _():
        for g in range(DEPTH - 1):
            fetch(g)
        whole.start()

    @pl.when(step < steps)
    def _():
        arrived(step)
        fetch(step + DEPTH - 1)
        wide[...] = raw[lax.rem(step, DEPTH)].astype(jnp.float32)
        for j in range(per_row):
            r_ref[:, j * 128:(j + 1) * 128] = wide[pl.ds(j, count, stride=per_row), :].astype(r_ref.dtype)

    @pl.when(step == steps)
    def _():
        for g in range(DEPTH - 1):
            arrived(steps + g)

    @pl.when(step == lag)
    def _():
        whole.wait()

    @pl.when(step >= lag)
    def _():
        factor = HEAD_DIM ** -0.5
        half = HEAD_DIM // 2

        def body(b, carry):
            for u in range(UNROLL):
                for i in range(SUB):
                    t = (b * UNROLL + u) * SUB + i
                    at = pl.multiple_of(slots[(step - lag) * TOK + t] * 8, 8)
                    spread[u, pl.ds(i * 8, 8), :] = store[pl.ds(at, 8), :]
            for u in range(UNROLL):
                here = pl.ds(pl.multiple_of((b * UNROLL + u) * SUB, SUB), SUB)
                cosines, sines = cos_ref[here, :], sin_ref[here, :]
                parts = [spread[u, pl.ds(j, SUB, stride=8), :] for j in range(6)]
                q_ref[here, :half] = ((parts[0] * cosines - parts[1] * sines) * factor).astype(q_ref.dtype)
                q_ref[here, half:] = ((parts[1] * cosines + parts[0] * sines) * factor).astype(q_ref.dtype)
                k_ref[here, :half] = (parts[2] * cosines - parts[3] * sines).astype(k_ref.dtype)
                k_ref[here, half:] = (parts[3] * cosines + parts[2] * sines).astype(k_ref.dtype)
                v_ref[here, :half] = parts[4].astype(v_ref.dtype)
                v_ref[here, half:] = parts[5].astype(v_ref.dtype)
            return carry

        lax.fori_loop(0, TOK // (SUB * UNROLL), body, 0)


def expand(group_size, lin, tiles, slots, cosines, sines):
    tokens = slots.shape[0] * slots.shape[1]
    width = tiles.shape[0] // (lin.shape[0] // 8) * 128
    steps, mine = tokens // TOK, tokens // group_size
    lag, count = LAG, mine // steps
    assert mine % steps == 0
    head = jax.ShapeDtypeStruct((tokens, HEAD_DIM), jnp.bfloat16)
    late = lambda i, s: (jnp.maximum(i - lag, 0), 0)
    return pl.pallas_call(
        functools.partial(expand_kernel, lag),
        grid_spec=pltpu.PrefetchScalarGridSpec(
            num_scalar_prefetch=1,
            grid=(steps + lag,),
            in_specs=[
                pl.BlockSpec(memory_space=pl.ANY),
                pl.BlockSpec(memory_space=pl.ANY),
                pl.BlockSpec((TOK, HEAD_DIM // 2), late),
                pl.BlockSpec((TOK, HEAD_DIM // 2), late),
            ],
            out_specs=[pl.BlockSpec((count, width), lambda i, s: (jnp.minimum(i, steps - 1), 0))] + [pl.BlockSpec((TOK, HEAD_DIM), late)] * 3,
            scratch_shapes=[
                pltpu.VMEM(lin.shape, lin.dtype),
                pltpu.VMEM((UNROLL, SUB * 8, 128), jnp.float32),
                pltpu.VMEM((DEPTH, count * width // 128, 128), tiles.dtype),
                pltpu.VMEM((count * width // 128, 128), jnp.float32),
                pltpu.SemaphoreType.DMA,
                pltpu.SemaphoreType.DMA((DEPTH,)),
            ],
        ),
        out_shape=(jax.ShapeDtypeStruct((mine, width), tiles.dtype),) + (head,) * 3,
        compiler_params=pltpu.CompilerParams(vmem_limit_bytes=VMEM_LIMIT),
        name="expand",
    )(slots.reshape(tokens), lin, tiles, cosines, sines)


def solution(mesh):
    group_size = mesh.shape["tp"]

    def local_step(token_ids, positions, table_rows, norm_scale, w_query, w_key, w_value):
        dev_index = lax.axis_index("tp")
        vocab_rows, model_width = table_rows.shape
        tokens = token_ids.shape[0]
        normalizer = float(np.asarray(math.sqrt(model_width), dtype=jnp.bfloat16))
        kv_heads = w_key.shape[1] // HEAD_DIM
        slot_count = max(kv_heads, group_size)
        slots_here = slot_count // group_size
        first_head = (dev_index * slots_here) // (slot_count // kv_heads)
        if kv_heads * HEAD_DIM == slots_here * HEAD_DIM:
            key_cols, value_cols = w_key, w_value
        else:
            key_cols = lax.dynamic_slice_in_dim(w_key, first_head * HEAD_DIM, slots_here * HEAD_DIM, axis=1)
            value_cols = lax.dynamic_slice_in_dim(w_value, first_head * HEAD_DIM, slots_here * HEAD_DIM, axis=1)

        plan = Plan(group_size, tokens, vocab_rows)
        slots, rows, counts, offsets, over = prepare(plan, group_size, vocab_rows, token_ids)
        fits = over[0] <= 0
        buf = gather_rows(plan, normalizer, counts, rows.reshape(-1), offsets, table_rows)
        _, lin, tiles, cosines, sines = multicast(plan, group_size, buf, norm_scale, w_query, key_cols, value_cols, positions)

        def fast(lin, tiles, cosines, sines):
            return expand(group_size, lin, tiles, slots, cosines, sines)

        def slow(lin, tiles, cosines, sines):
            return dense_path(group_size, token_ids, positions, table_rows, norm_scale, w_query, key_cols, value_cols)

        residual, queries, key_heads, value_heads = lax.cond(fits, fast, slow, lin, tiles, cosines, sines)
        return residual, queries[:, None, :], key_heads[:, None, :], value_heads[:, None, :]

    head_spec = P("dp", "tp", None)
    return jax.shard_map(local_step, mesh=mesh, in_specs=(P("dp"), P("dp"), P("tp", None), P(), P(None, "tp"), P(), P()), out_specs=(P(("dp", "tp"), None), head_spec, head_spec, head_spec), check_vma=False)
```

profile of v0, /device:TPU:125, one launch (start us, length us, event | category | flops | bytes accessed | tf_op | source)
XLA Modules:
  0.0 213.1 jit_solution(779078012445952633)
XLA Ops:
  0.6 2.9 %slots.1 = (s32[64,128]{1,0:T(8,128)S(1)}, s32[24,128]{1,0:T(8,128)}, s32[8,128]{1,0:T(8,128)}, f32[128,128]{1,0:T(8,128)}, s32[1]{0:T(128)}) custom-call(s32[64,128]{1,0:T(8,128)} %bitcast.30), custom_call_target="tpu_custom_call" | custom-call | tf_op jit(solution)/shard_map/slots/pallas_call | solution.py:153
  3.5 0.0 copy-start.1
  3.5 0.0 copy-start.3
  3.5 0.0 copy-start.4
  3.5 0.0 copy-start.6
  3.6 0.0 copy-start.8
  3.6 12.2 %owner_rows.1.buf_in = bf16[6016,2048]{1,0:T(8,128)(2,1)} custom-call(s32[8,128]{1,0:T(8,128)} %get-tuple-element.62.counts, s32[3072]{0:T(1024)} %bitcast.33, f32[128,128]{1,0:T(8,128)} %get-tuple-element.64.offsets, bf16[32152,2048]{1,0:T(8,128)(2,1)} %table.1), custom_call_target="tpu_custom_call" | custom-call | flops 2952790016 | bytes 100000000 | tf_op jit(solution)/shard_map/owner_rows/pallas_call | solution.py:285
  15.8 0.5 multiply_power_fusion.1.freq_ref
  16.3 0.0 copy-done.1
  16.3 0.0 copy-done.3
  16.3 0.0 copy-done.4
  16.3 0.0 copy-done.6
  16.3 0.0 copy-done.8
  16.3 0.0 copy-start
  16.3 162.0 %multicast.1 = (bf16[6016,2048]{1,0:T(8,128)(2,1)}, f32[48128,128]{1,0:T(8,128)}, bf16[96256,128]{1,0:T(8,128)(2,1)}, f32[8192,128]{1,0:T(8,128)}, f32[8192,128]{1,0:T(8,128)}) custom-call(bf16[6016,2048]{1,0:T(8,128)(2,1)} %owner_rows.1.buf_in, f32[1,2048]{1,0:T(1,128)S(1)} %bitcast.34, ...), custom_call_target="tpu_custom_call", output_to_operand_aliasing={{0}: (0, {})} | custom-call | flops 99999997952 | bytes 100000000 | tf_op jit(solution)/shard_map/multicast/pallas_call | solution.py:561
  179.0 0.0 copy-done
  179.0 33.9 %conditional.1 = (bf16[1024,2048]{1,0:T(8,128)(2,1)}, bf16[8192,1,256]{2,0,1:T(8,128)(2,1)}, bf16[8192,1,256]{2,0,1:T(8,128)(2,1)}, bf16[8192,1,256]{2,0,1:T(8,128)(2,1)}) conditional(s32[]{:T(128)} %bitcast.12, (s32[8192]{0:T(1024)S(1)}, bf16[32152,2048]{1,0:T(8,128)(2,1)}, f32[2048]{0:T(1024)S(1)}, bf16[2048,256]{1,0:T(8,128)(2,1)}, ...), branch_computations={%region_0.3_spmd, %region_3.4_spmd} | conditional | flops 25873674240 | bytes 695641216 | solution.py:719
  179.2 33.7 %expand.1 = (bf16[1024,2048]{1,0:T(8,128)(2,1)}, bf16[8192,256]{1,0:T(8,128)(2,1)}, bf16[8192,256]{1,0:T(8,128)(2,1)}, bf16[8192,256]{1,0:T(8,128)(2,1)}) custom-call(s32[8192]{0:T(1024)S(1)} %bitcast.31, f32[48128,128]{1,0:T(8,128)} %get-tuple-element.39.lin, bf16[96256,128]{1,0:T(8,128)(2,1)} %get-tuple-element.40.tiles, ...), custom_call_target="tpu_custom_call" | custom-call | tf_op jit(solution)/shard_map/cond/branch_1_fun/expand/pallas_call | solution.py:662
Async XLA Ops:
  3.5 12.8 %copy-start.1 = (s32[8192]{0:T(1024)S(1)}, s32[8192]{0:T(1024)}, u32[]{:S(2)}) copy-start(s32[8192]{0:T(1024)} %param.10) | copy-start | bytes 98308
  3.5 12.8 %copy-start.3 = (f32[2048]{0:T(1024)S(1)}, f32[2048]{0:T(1024)}, u32[]{:S(2)}) copy-start(f32[2048]{0:T(1024)} %param.12) | copy-start | bytes 24580
  3.5 12.8 %copy-start.4 = (bf16[2048,256]{1,0:T(8,128)(2,1)S(1)}, bf16[2048,256]{1,0:T(8,128)(2,1)}, u32[]{:S(2)}) copy-start(bf16[2048,256]{1,0:T(8,128)(2,1)} %wq_ref.1) | copy-start | bytes 3145732
  3.5 12.8 %copy-start.6 = (bf16[2048,256]{1,0:T(8,128)(2,1)S(1)}, bf16[2048,256]{1,0:T(8,128)(2,1)}, u32[]{:S(2)}) copy-start(bf16[2048,256]{1,0:T(8,128)(2,1)} %wk_ref.1) | copy-start | bytes 3145732
  3.6 12.8 %copy-start.8 = (bf16[2048,256]{1,0:T(8,128)(2,1)S(1)}, bf16[2048,256]{1,0:T(8,128)(2,1)}, u32[]{:S(2)}) copy-start(bf16[2048,256]{1,0:T(8,128)(2,1)} %wv_ref.1) | copy-start | bytes 3145732
  16.3 162.6 %copy-start = (s32[8192]{0:T(1024)S(1)}, s32[8192]{0:T(1024)}, u32[]{:S(2)}) copy-start(s32[8192]{0:T(1024)} %param.9) | copy-start | bytes 98308
where the time goes:
time: 215 us; the launch traced here: 213 us
  Pallas kernels  211 us (98%)
    pallas_call x1, Pallas kernels, multicast(): pl.pallas_call(functools.partial(multicast_kernel, plan, group_size), out...  162 us
    pallas_call x1, Pallas kernels, expand(): pl.pallas_call(functools.partial(expand_kernel, lag), grid_spec=pltpu.Pre...  33.7 us
    pallas_call x1, Pallas kernels, gather_rows(): pl.pallas_call(functools.partial(gather_kernel, plan, normalizer), out_sh...  12.2 us

commit v1 on v0

--- a/solution.py
+++ b/solution.py
@@ -207,11 +207,10 @@
             self.wait(groups + g)
 
 
-def gather_kernel(plan, normalizer, counts, rows_smem, offsets, table, out, slabs, stage, hot_in, hot_out, sem, out_sem, hot_sem):
+def gather_kernel(plan, counts, rows_smem, offsets, table, out, slabs, stage, sem, out_sem):
     me = lax.axis_index("tp")
     total = jnp.minimum(counts[me, 0], choose(plan.caps, me))
     base = choose(plan.bases, me)
-    scale = jnp.float32(normalizer)
     groups = (total + PICK - 1) // PICK
     picker = Picker(rows_smem, 0, groups, offsets, table, slabs, sem)
     picker.lead()
@@ -223,55 +222,16 @@
         def _():
             pltpu.make_async_copy(stage.at[side], out.at[pl.ds(0, PICK)], out_sem.at[side]).wait()
 
-        stage[side] = (picked * scale).astype(jnp.bfloat16)
+        stage[side] = picked.astype(stage.dtype)
         at = pl.multiple_of(base + g * PICK, PICK)
         pltpu.make_async_copy(stage.at[side], out.at[pl.ds(at, PICK)], out_sem.at[side]).start()
 
-    step = hot_in.shape[1]
-    hot_steps = jnp.where(me == 0, plan.hot // step, 0)
-
-    def load(i):
-        return pltpu.make_async_copy(table.at[pl.ds(pl.multiple_of(i * step, step), step)], hot_in.at[lax.rem(i, 2)], hot_sem.at[lax.rem(i, 2)])
-
-    def save(i):
-        return pltpu.make_async_copy(hot_out.at[lax.rem(i, 2)], out.at[pl.ds(pl.multiple_of(i * step, step), step)], hot_sem.at[2 + lax.rem(i, 2)])
-
-    def hot_turn(i):
-        @pl.when(i < hot_steps)
-        def _():
-            load(i).wait()
-
-            @pl.when(i >= 2)
-            def _():
-                save(i - 2).wait()
-            hot_out[lax.rem(i, 2)] = (hot_in[lax.rem(i, 2)].astype(jnp.float32) * scale).astype(jnp.bfloat16)
-            save(i).start()
-
-            @pl.when(i + 2 < hot_steps)
-            def _():
-                load(i + 2).start()
-
-    for i in range(2):
-        @pl.when(i < hot_steps)
-        def _():
-            load(jnp.int32(i)).start()
-
-    def rest(i, carry):
-        hot_turn(i)
-        return carry
-
     def body(g, carry):
         emit(g, picker.turn(g))
-        hot_turn(g)
         return carry
 
     lax.fori_loop(0, groups, body, 0)
-    lax.fori_loop(groups, jnp.maximum(hot_steps, groups), rest, 0)
     picker.drain(groups)
-    for back in (2, 1):
-        @pl.when(hot_steps >= back)
-        def _():
-            save(hot_steps - back).wait()
     for last in (2, 1):
         @pl.when(groups >= last)
         def _():
@@ -279,22 +239,18 @@
             pltpu.make_async_copy(stage.at[side], out.at[pl.ds(0, PICK)], out_sem.at[side]).wait()
 
 
-def gather_rows(plan, normalizer, counts, rows, offsets, table):
+def gather_rows(plan, counts, rows, offsets, table):
     width = table.shape[1]
-    hot_step = CHUNK
     return pl.pallas_call(
-        functools.partial(gather_kernel, plan, normalizer),
+        functools.partial(gather_kernel, plan),
         out_shape=jax.ShapeDtypeStruct((plan.rows, width), table.dtype),
         in_specs=[pl.BlockSpec(memory_space=pltpu.SMEM), pl.BlockSpec(memory_space=pltpu.SMEM), pl.BlockSpec(memory_space=pltpu.VMEM), pl.BlockSpec(memory_space=pl.ANY)],
         out_specs=pl.BlockSpec(memory_space=pl.ANY),
         scratch_shapes=[
             pltpu.VMEM((DEPTH, PICK * SLAB, width), table.dtype),
             pltpu.VMEM((2, PICK, width), table.dtype),
-            pltpu.VMEM((2, hot_step, width), table.dtype),
-            pltpu.VMEM((2, hot_step, width), table.dtype),
             pltpu.SemaphoreType.DMA((DEPTH,)),
             pltpu.SemaphoreType.DMA((2,)),
-            pltpu.SemaphoreType.DMA((4,)),
         ],
         compiler_params=pltpu.CompilerParams(vmem_limit_bytes=VMEM_LIMIT),
         cost_estimate=pl.CostEstimate(flops=2 * 2048 * 256 * 2816, bytes_accessed=100_000_000, transcendentals=0),
@@ -326,7 +282,7 @@
     return jnp.where(((quarter + 1) & 2) == 2, -first, first), jnp.where((quarter & 2) == 2, -second, second)
 
 
-def multicast_kernel(plan, group_size, buf_in, scale_ref, wq_ref, wk_ref, wv_ref, pos_ref, freq_ref, buf, lin, tiles, cos_out, sin_out, got, ring_sem, pair_sem, fresh, made, wide, tiled, turned, in_sem, out_sem, tile_sem, turn_sem):
+def multicast_kernel(plan, group_size, normalizer, buf_in, table, scale_ref, wq_ref, wk_ref, wv_ref, pos_ref, freq_ref, buf, lin, tiles, cos_out, sin_out, got, ring_sem, pair_sem, fresh, made, wide, tiled, turned, in_sem, out_sem, tile_sem, turn_sem):
     del buf_in
     chips = group_size // CORES
     me = lax.axis_index("tp")
@@ -357,11 +313,11 @@
     def rows(j):
         return pl.ds(pl.multiple_of(j * CHUNK, CHUNK), CHUNK)
 
-    def ring(j):
-        return pltpu.make_async_remote_copy(src_ref=buf.at[rows(j)], dst_ref=buf.at[rows(j)], send_sem=ring_sem.at[j], recv_sem=got.at[j], device_id={"tp": ahead}, device_id_type=pl.DeviceIdType.MESH)
-
-    def pair(j):
-        return pltpu.make_async_remote_copy(src_ref=buf.at[rows(j)], dst_ref=buf.at[rows(j)], send_sem=pair_sem.at[j], recv_sem=got.at[j], device_id={"tp": mate}, device_id_type=pl.DeviceIdType.MESH)
+    def ring(j, source=buf):
+        return pltpu.make_async_remote_copy(src_ref=source.at[rows(j)], dst_ref=buf.at[rows(j)], send_sem=ring_sem.at[j], recv_sem=got.at[j], device_id={"tp": ahead}, device_id_type=pl.DeviceIdType.MESH)
+
+    def pair(j, source=buf):
+        return pltpu.make_async_remote_copy(src_ref=source.at[rows(j)], dst_ref=buf.at[rows(j)], send_sem=pair_sem.at[j], recv_sem=got.at[j], device_id={"tp": mate}, device_id_type=pl.DeviceIdType.MESH)
 
     def loop(count, fn):
         def body(t, c):
@@ -378,8 +334,22 @@
     def _():
         loop(my_turn, lambda t: pair(cross_at + t).start())
 
-    loop(mine, lambda t: ring(mine_at + t).start())
-    loop(mine, lambda t: pair(mine_at + t).start())
+    hot_chunks = plan.hot // CHUNK
+    assert half[0] >= hot_chunks
+
+    def start(copy, j):
+        from_table = (me == 0) & (j < hot_chunks)
+
+        @pl.when(from_table)
+        def _():
+            copy(j, table).start()
+
+        @pl.when(jnp.logical_not(from_table))
+        def _():
+            copy(j, buf).start()
+
+    loop(mine, lambda t: start(ring, mine_at + t))
+    loop(mine, lambda t: start(pair, mine_at + t))
 
     @pl.when(core == 1)
     def _():
@@ -413,9 +383,9 @@
         cross, _ = arrival(t, -step, 1 - core)
         return jnp.where(local, home(s, 0), come), jnp.where(local, home(s, 1), cross)
 
-    def load(s, side, j):
+    def load(s, side, j, source=buf):
         place = lax.rem(s, 2)
-        return pltpu.make_async_copy(buf.at[rows(j)], fresh.at[place, pl.ds(side * CHUNK, CHUNK)], in_sem.at[place, side])
+        return pltpu.make_async_copy(source.at[rows(j)], fresh.at[place, pl.ds(side * CHUNK, CHUNK)], in_sem.at[place, side])
 
     def save(s, side, j):
         place = lax.rem(s, 2)
@@ -441,7 +411,7 @@
             save(s, 1, 0).wait()
             lay(s, 0, 0).wait()
             lay(s, 1, 0).wait()
-        came = fresh[place]
+        came = (fresh[place].astype(jnp.float32) * normalizer).astype(buf.dtype)
         for j in range(per_row):
             wide[pl.ds(j, width, stride=per_row), :] = came[:, j * 128:(j + 1) * 128].astype(jnp.float32)
         tiled[place] = wide[...].astype(tiled.dtype)
@@ -504,8 +474,8 @@
                 ring(one).start()
             pair(one).start()
             pair(two).wait_recv()
-        load(s, 0, one).start()
-        load(s, 1, two).start()
+        start(functools.partial(load, s, 0), one)
+        start(functools.partial(load, s, 1), two)
 
         @pl.when(s >= 1)
         def _():
@@ -552,16 +522,16 @@
         loop(count, left)
 
 
-def multicast(plan, group_size, buf, norm_scale, w_query, key_cols, value_cols, positions):
+def multicast(plan, group_size, normalizer, buf, table_rows, norm_scale, w_query, key_cols, value_cols, positions):
     chunks, width = plan.rows // CHUNK, buf.shape[1]
     per_row = width // 128
     tokens, half = positions.shape[0], HEAD_DIM // 2
     table = jax.ShapeDtypeStruct((tokens, half), jnp.float32)
     vmem = pl.BlockSpec(memory_space=pltpu.VMEM)
     return pl.pallas_call(
-        functools.partial(multicast_kernel, plan, group_size),
+        functools.partial(multicast_kernel, plan, group_size, normalizer),
         out_shape=(jax.ShapeDtypeStruct(buf.shape, buf.dtype), jax.ShapeDtypeStruct((plan.rows * 8, 128), jnp.float32), jax.ShapeDtypeStruct((plan.rows * per_row, 128), buf.dtype), table, table),
-        in_specs=[pl.BlockSpec(memory_space=pl.ANY)] + [vmem] * 6,
+        in_specs=[pl.BlockSpec(memory_space=pl.ANY)] * 2 + [vmem] * 6,
         out_specs=(pl.BlockSpec(memory_space=pl.ANY),) * 5,
         scratch_shapes=[
             pltpu.SemaphoreType.DMA((chunks,)),
@@ -581,7 +551,7 @@
         compiler_params=pltpu.CompilerParams(collective_id=0, has_side_effects=True, vmem_limit_bytes=VMEM_LIMIT),
         cost_estimate=pl.CostEstimate(flops=100_000_000_000, bytes_accessed=100_000_000, transcendentals=0),
         name="multicast",
-    )(buf, norm_scale.reshape(1, width), w_query, key_cols, value_cols, positions.reshape(-1, 128), inverse_freq().reshape(1, half))
+    )(buf, table_rows, norm_scale.reshape(1, width), w_query, key_cols, value_cols, positions.reshape(-1, 128), inverse_freq().reshape(1, half))
 
 
 def expand_kernel(lag, slots, lin, tiles, cos_ref, sin_ref, r_ref, q_ref, k_ref, v_ref, store, spread, raw, wide, sem, fetch_sem):
@@ -707,8 +677,8 @@
         plan = Plan(group_size, tokens, vocab_rows)
         slots, rows, counts, offsets, over = prepare(plan, group_size, vocab_rows, token_ids)
         fits = over[0] <= 0
-        buf = gather_rows(plan, normalizer, counts, rows.reshape(-1), offsets, table_rows)
-        _, lin, tiles, cosines, sines = multicast(plan, group_size, buf, norm_scale, w_query, key_cols, value_cols, positions)
+        buf = gather_rows(plan, counts, rows.reshape(-1), offsets, table_rows)
+        _, lin, tiles, cosines, sines = multicast(plan, group_size, normalizer, buf, table_rows, norm_scale, w_query, key_cols, value_cols, positions)
 
         def fast(lin, tiles, cosines, sines):
             return expand(group_size, lin, tiles, slots, cosines, sines)

time: 215 us -> 213 us (level)
  no operation moved by 1% of the time
where the time goes in v1:
time: 213 us
  Pallas kernels  210 us (99%)
    pallas_call x1, Pallas kernels, multicast(): pl.pallas_call(functools.partial(multicast_kernel, plan, group_size, norm...  166 us
    pallas_call x1, Pallas kernels, expand(): pl.pallas_call(functools.partial(expand_kernel, lag), grid_spec=pltpu.Pre...  33.7 us
    pallas_call x1, Pallas kernels, gather_rows(): pl.pallas_call(functools.partial(gather_kernel, plan), out_shape=jax.Shap...  7.49 us

profile of v1, /device:TPU:125, one launch (start us, length us, event | category | flops | bytes accessed | tf_op | source)
XLA Modules:
  0.0 212.9 jit_solution(15711178217023330286)
XLA Ops:
  0.6 2.9 %slots.1 = (s32[64,128]{1,0:T(8,128)S(1)}, s32[24,128]{1,0:T(8,128)}, s32[8,128]{1,0:T(8,128)}, f32[128,128]{1,0:T(8,128)}, s32[1]{0:T(128)}) custom-call(s32[64,128]{1,0:T(8,128)} %bitcast.30), custom_call_target="tpu_custom_call" | custom-call | tf_op jit(solution)/shard_map/slots/pallas_call | solution.py:153
  3.5 0.0 copy-start.1
  3.5 0.0 copy-start.3
  3.5 0.0 copy-start.4
  3.5 0.0 copy-start.6
  3.6 0.0 copy-start.8
  3.6 7.5 %owner_rows.1.buf_in = bf16[6016,2048]{1,0:T(8,128)(2,1)} custom-call(s32[8,128]{1,0:T(8,128)} %get-tuple-element.62.counts, s32[3072]{0:T(1024)} %bitcast.33, f32[128,128]{1,0:T(8,128)} %get-tuple-element.64.offsets, bf16[32152,2048]{1,0:T(8,128)(2,1)} %table.3), custom_call_target="tpu_custom_call" | custom-call | flops 2952790016 | bytes 100000000 | tf_op jit(solution)/shard_map/owner_rows/pallas_call | solution.py:244
  11.1 0.5 multiply_power_fusion.1.freq_ref
  11.6 0.0 copy-done.1
  11.6 0.0 copy-done.3
  11.6 0.0 copy-done.4
  11.6 0.0 copy-done.6
  11.6 0.0 copy-done.8
  11.6 0.0 copy-start
  11.6 166.5 %multicast.1 = (bf16[6016,2048]{1,0:T(8,128)(2,1)}, f32[48128,128]{1,0:T(8,128)}, bf16[96256,128]{1,0:T(8,128)(2,1)}, f32[8192,128]{1,0:T(8,128)}, f32[8192,128]{1,0:T(8,128)}) custom-call(bf16[6016,2048]{1,0:T(8,128)(2,1)} %owner_rows.1.buf_in, bf16[32152,2048]{1,0:T(8,128)(2,1)} %table.3, f32[1,2048]{1,0:T(1,128)S(1)} %bitcast.34, ...), custom_call_target="tpu_custom_call", output_to_operand_aliasing={{0}: (0, {})} | custom-call | flops 99999997952 | bytes 100000000 | tf_op jit(solution)/shard_map/multicast/pallas_call | solution.py:531
  178.7 0.0 copy-done
  178.8 33.9 %conditional.1 = (bf16[1024,2048]{1,0:T(8,128)(2,1)}, bf16[8192,1,256]{2,0,1:T(8,128)(2,1)}, bf16[8192,1,256]{2,0,1:T(8,128)(2,1)}, bf16[8192,1,256]{2,0,1:T(8,128)(2,1)}) conditional(s32[]{:T(128)} %bitcast.12, (s32[8192]{0:T(1024)S(1)}, bf16[32152,2048]{1,0:T(8,128)(2,1)}, f32[2048]{0:T(1024)S(1)}, bf16[2048,256]{1,0:T(8,128)(2,1)}, ...), branch_computations={%region_0.3_spmd, %region_3.4_spmd} | conditional | flops 25873674240 | bytes 695641216 | solution.py:689
  179.0 33.7 %expand.1 = (bf16[1024,2048]{1,0:T(8,128)(2,1)}, bf16[8192,256]{1,0:T(8,128)(2,1)}, bf16[8192,256]{1,0:T(8,128)(2,1)}, bf16[8192,256]{1,0:T(8,128)(2,1)}) custom-call(s32[8192]{0:T(1024)S(1)} %bitcast.31, f32[48128,128]{1,0:T(8,128)} %get-tuple-element.39.lin, bf16[96256,128]{1,0:T(8,128)(2,1)} %get-tuple-element.40.tiles, ...), custom_call_target="tpu_custom_call" | custom-call | tf_op jit(solution)/shard_map/cond/branch_1_fun/expand/pallas_call | solution.py:632
Async XLA Ops:
  3.5 8.1 %copy-start.1 = (s32[8192]{0:T(1024)S(1)}, s32[8192]{0:T(1024)}, u32[]{:S(2)}) copy-start(s32[8192]{0:T(1024)} %param.10) | copy-start | bytes 98308
  3.5 8.1 %copy-start.3 = (f32[2048]{0:T(1024)S(1)}, f32[2048]{0:T(1024)}, u32[]{:S(2)}) copy-start(f32[2048]{0:T(1024)} %param.12) | copy-start | bytes 24580
  3.5 8.1 %copy-start.4 = (bf16[2048,256]{1,0:T(8,128)(2,1)S(1)}, bf16[2048,256]{1,0:T(8,128)(2,1)}, u32[]{:S(2)}) copy-start(bf16[2048,256]{1,0:T(8,128)(2,1)} %wq_ref.1) | copy-start | bytes 3145732
  3.5 8.1 %copy-start.6 = (bf16[2048,256]{1,0:T(8,128)(2,1)S(1)}, bf16[2048,256]{1,0:T(8,128)(2,1)}, u32[]{:S(2)}) copy-start(bf16[2048,256]{1,0:T(8,128)(2,1)} %wk_ref.1) | copy-start | bytes 3145732
  3.6 8.1 %copy-start.8 = (bf16[2048,256]{1,0:T(8,128)(2,1)S(1)}, bf16[2048,256]{1,0:T(8,128)(2,1)}, u32[]{:S(2)}) copy-start(bf16[2048,256]{1,0:T(8,128)(2,1)} %wv_ref.1) | copy-start | bytes 3145732
  11.6 167.1 %copy-start = (s32[8192]{0:T(1024)S(1)}, s32[8192]{0:T(1024)}, u32[]{:S(2)}) copy-start(s32[8192]{0:T(1024)} %param.9) | copy-start | bytes 98308
